TPU v7x, 32 devices: a whole 2x2x4 slice. The times are simulated.
32 devices in a mesh: freq: 16 (over z, y, x), depth: 2 (over core).
Axes of the slice: x: 2, y: 2, z: 4, core: 2. Of those that a mesh axis runs over, the one named last changes fastest.
Arguments:
- pressure_field: bfloat16 [8192, 4096], P('depth', 'freq'), may hold values from -6 to 6
- block_main: bfloat16 [8192, 3, 2, 128], P('depth'), may hold values from -0.15625 to 0.15625
- block_coupled: bfloat16 [8192, 3, 2, 128], P('depth'), may hold values from -0.15625 to 0.15625
- coupling: float32 [4096], P('freq'), may hold values from -3 to 3
- frequencies: float32 [2048], replicated, may hold values from 1 to 1024
- receivers: int32 [512], replicated, may hold values from 0 to 8191
- floors: int32 [4], replicated, may hold values from 2048 to 8191
Outputs:
- series: float32 [512, 2048], P('depth', 'freq')
Inputs may be any that keep to these rules, and one draw needn't show every extreme that they name: `receivers`: any depth cells, repeats possible.
All inputs are finite; a program needn't handle non-finite values.
Results may differ from a plain program's by a relative error of at most 0.0061.
Values may be sent and summed in bfloat16 or wider, within the bound.
A program may use at most 256 MiB of HBM per device.

v0:
```python
import math

import jax
import jax.numpy as jnp
from jax import lax
from jax.sharding import PartitionSpec as P

NT = 2048
STEPS = 4


def padded_2(cells, sides, width):
    for axis, dim in sides:
        count = lax.axis_size(axis)
        ends = count - 1
        head = lax.slice_in_dim(cells, 0, width, axis=dim)
        tail = lax.slice_in_dim(cells, cells.shape[dim] - width, cells.shape[dim], axis=dim)
        cells = jnp.concatenate(
            [
                lax.ppermute(tail, axis, [(i, (i + 1) % count) for i in range(ends)]),
                cells,
                lax.ppermute(head, axis, [((i + 1) % count, i) for i in range(ends)]),
            ],
            axis=dim,
        )
    return cells


def times_unit(values):
    column = lax.broadcasted_iota(jnp.int32, values.shape, 1)
    upper = jnp.roll(values, -1, axis=1)
    lower = jnp.roll(values, 1, axis=1)
    return jnp.where(column % 2 == 0, -upper, lower)


def order_blocks(blocks, block_count, block_size):
    shaped = blocks.reshape(block_count, block_size, 3, 2, block_size)
    return shaped.transpose(0, 2, 3, 1, 4).reshape(block_count, 3, 2 * block_size, block_size)


def apply_blocks(ordered, padded, block_count, block_size):
    width = padded.shape[1]
    stacked = padded.reshape(block_count + 2, block_size, width)
    product = jnp.zeros((block_count, 2 * block_size, width), jnp.float32)
    for offset in range(3):
        product = product + jnp.einsum(
            "bij,bjc->bic",
            ordered[:, offset],
            stacked[offset : offset + block_count],
            preferred_element_type=jnp.float32,
        )
    real_part = product[:, :block_size].reshape(block_count * block_size, width)
    imag_part = product[:, block_size:].reshape(block_count * block_size, width)
    return real_part + times_unit(imag_part)


def make_basis(freq_values, sample_times):
    phase = jnp.mod(freq_values[:, None] * sample_times[None, :], jnp.float32(NT)) / jnp.float32(NT)
    angle = 2.0 * math.pi * phase
    stacked = jnp.stack([jnp.cos(angle), -jnp.sin(angle)], axis=1)
    return stacked.reshape(2 * freq_values.shape[0], sample_times.shape[0]).astype(jnp.bfloat16)


def local(pressure_field, block_main, block_coupled, coupling, frequencies, receivers, floors):
    rows_here = pressure_field.shape[0]
    block_size = block_main.shape[3]
    block_count = rows_here // block_size
    main_blocks = order_blocks(block_main, block_count, block_size)
    side_blocks = order_blocks(block_coupled, block_count, block_size)
    width = pressure_field.shape[1]
    column = jnp.arange(width, dtype=jnp.int32)
    even_weight = jnp.take(coupling, column - column % 2)
    odd_weight = jnp.take(coupling, column - column % 2 + 1)
    first_row = lax.axis_index("depth") * rows_here
    depth_index = first_row + jnp.arange(rows_here, dtype=jnp.int32)
    columns = pressure_field
    for step in range(STEPS):
        padded = padded_2(columns, (("depth", 0),), block_size)
        coupled = apply_blocks(side_blocks, padded, block_count, block_size)
        combined = (
            apply_blocks(main_blocks, padded, block_count, block_size)
            + even_weight[None, :] * coupled
            + odd_weight[None, :] * times_unit(coupled)
        )
        damping = jnp.where(depth_index >= floors[step], 0.5, 1.0).astype(jnp.float32)
        columns = (damping[:, None] * combined).astype(jnp.bfloat16)
    local_index = receivers - first_row
    selector = (local_index[:, None] == jnp.arange(rows_here, dtype=jnp.int32)[None, :]).astype(
        jnp.bfloat16
    )
    picked = jnp.dot(selector, columns, preferred_element_type=jnp.float32).astype(jnp.bfloat16)
    total_freq = frequencies.shape[0]
    factor = 1.0 / math.sqrt(total_freq)
    owned = lax.psum_scatter(
        picked.astype(jnp.float32).astype(jnp.bfloat16), "depth", scatter_dimension=0, tiled=True
    )
    time_here = NT // lax.axis_size("freq")
    sample_times = (
        lax.axis_index("freq") * time_here + jnp.arange(time_here, dtype=jnp.int32)
    ).astype(jnp.float32)
    entries = make_basis(frequencies, sample_times)
    summed = jnp.dot(
        lax.all_gather(owned, "freq", axis=1, tiled=True),
        entries,
        preferred_element_type=jnp.float32,
    )
    return summed * factor


def solution(mesh):
    in_specs = (
        P("depth", "freq"),
        P("depth", None, None, None),
        P("depth", None, None, None),
        P("freq"),
        P(),
        P(),
        P(),
    )
    out_specs = P("depth", "freq")
    return jax.shard_map(local, mesh=mesh, in_specs=in_specs, out_specs=out_specs, check_vma=False)
```

profile of v0, /device:TPU:0, one launch (start us, length us, event | category | flops | bytes accessed | tf_op | source)
XLA Modules:
  0.0 554.3 jit_solution(17722406453393507542)
XLA Ops:
  20.9 6.9 %copy.14 = bf16[32,128,3,2,128]{4,1,3,0,2:T(8,128)(2,1)S(1)} copy(bf16[32,128,3,2,128]{4,3,2,1,0:T(2,128)(2,1)} %bitcast.282) | data formatting | bytes 12582912 | tf_op jit(solution)/shard_map/reshape | solution.py:37
  50.8 7.0 %bitcast_add_fusion = f32[32,256,256]{2,1,0:T(8,128)S(1)} fusion(f32[32,256,256]{2,1,0:T(8,128)} %fusion.93, f32[32,256,256]{1,2,0:T(8,128)} %fusion.86, bf16[32,128,256]{2,1,0:T(8,128)(2,1)S(1)} %bitcast.249, bf16[32,3,256,128]{3,2,0,1:T(8,128)(2,1)S(1)} %bitcast.197), kind=kOutput, calls=%fused_computation.2 | convolution fusion | flops 541065216 | bytes 29360128 | tf_op jit(solution)/shard_map/bij,bjc->bic/dot_general | solution.py:46
  86.7 10.7 %bitcast_add_fusion.2 = f32[32,256,256]{2,1,0:T(8,128)} fusion(f32[32,256,256]{2,1,0:T(8,128)} %fusion.82, f32[32,256,256]{1,2,0:T(8,128)} %fusion.75, bf16[32,128,256]{2,1,0:T(8,128)(2,1)S(1)} %bitcast.250, bf16[32,3,256,128]{3,2,0,1:T(8,128)(2,1)S(1)} %bitcast.185), kind=kOutput, calls=%fused_computation.4 | convolution fusion | flops 541065216 | bytes 29360128 | tf_op jit(solution)/shard_map/bij,bjc->bic/dot_general | solution.py:46
  97.4 6.2 %fusion.125 = (f32[32,128,256]{2,1,0:T(8,128)}, f32[32,128,256]{2,1,0:T(8,128)S(1)}) fusion(f32[32,256,256]{2,1,0:T(8,128)} %bitcast_add_fusion.2), kind=kLoop, calls=%fused_computation.193 | loop fusion | bytes 16777216 | tf_op jit(solution)/shard_map/slice | solution.py:52
  111.9 16.2 %fusion.16 = bf16[32,128,256]{2,1,0:T(8,128)(2,1)} fusion(f32[32,128,1]{2,1,0:T(8,128)} %bitcast.270, f32[32,128,255]{2,1,0:T(8,128)} %bitcast.238, f32[32,128,255]{2,1,0:T(8,128)} %bitcast.237, f32[32,128,1]{2,1,0:T(8,128)} %bitcast.269, f32[32,128,1]{2,1,0:T(8,128)} %bitcast.256, f32[32,128,255]{2,1,0:T(8,128)} %bitcast.224, ...), kind=kLoop, calls=%fused_computation.33 | loop fusion | flops 23068672 | bytes 35672320 | tf_op jit(solution)/shard_map/convert_element_type | solution.py:86
  128.1 6.3 %fusion.90 = f32[32,256,256]{1,2,0:T(8,128)} fusion(bf16[32,128,256]{2,1,0:T(8,128)(2,1)} %fusion.16, bf16[32,3,256,128]{3,2,0,1:T(8,128)(2,1)S(1)} %bitcast.198), kind=kOutput, calls=%fused_computation.141 | convolution fusion | flops 536870912 | bytes 12582912 | tf_op jit(solution)/shard_map/bij,bjc->bic/dot_general | solution.py:46
  134.5 10.6 %fusion.6 = bf16[4096,256]{1,0:T(8,128)(2,1)} fusion(f32[4096,1]{1,0:T(8,128)} %get-tuple-element.67, f32[4096,255]{1,0:T(8,128)} %get-tuple-element.69, f32[4096,255]{1,0:T(8,128)} %get-tuple-element.68, f32[4096,1]{1,0:T(8,128)} %get-tuple-element.66, f32[4096,1]{1,0:T(8,128)} %get-tuple-element.59, f32[4096,255]{1,0:T(8,128)S(1)} %copy-done.18, ...), kind=kLoop, calls=%fused_computation.20 | loop fusion | flops 17825792 | bytes 27283712 | tf_op jit(solution)/shard_map/convert_element_type | solution.py:86
  150.4 6.2 %fusion.79 = f32[32,256,256]{1,2,0:T(8,128)} fusion(bf16[32,128,256]{2,1,0:T(8,128)(2,1)} %fusion.16, bf16[32,3,256,128]{3,2,0,1:T(8,128)(2,1)S(1)} %bitcast.186), kind=kOutput, calls=%fused_computation.130 | convolution fusion | flops 536870912 | bytes 12582912 | tf_op jit(solution)/shard_map/bij,bjc->bic/dot_general | solution.py:46
  158.2 5.4 fusion.87
  164.4 8.6 %add_bitcast_fusion.4 = f32[32,256,256]{2,1,0:T(8,128)} fusion(f32[32,256,256]{1,2,0:T(8,128)} %fusion.87, f32[32,256,256]{1,2,0:T(8,128)S(1)} %bitcast.244, bf16[32,128,256]{2,1,0:T(8,128)(2,1)} %bitcast.251, bf16[32,3,256,128]{3,2,0,1:T(8,128)(2,1)S(1)} %bitcast.200), kind=kOutput, calls=%fused_computation.10 | convolution fusion | flops 541065216 | bytes 29360128 | tf_op jit(solution)/shard_map/bij,bjc->bic/dot_general | solution.py:46
  173.0 6.3 %fusion.124 = (f32[32,128,256]{2,1,0:T(8,128)}, f32[32,128,256]{2,1,0:T(8,128)S(1)}) fusion(f32[32,256,256]{2,1,0:T(8,128)} %add_bitcast_fusion.4), kind=kLoop, calls=%fused_computation.192 | loop fusion | bytes 16777216 | tf_op jit(solution)/shard_map/slice | solution.py:52
  203.8 10.3 %add_bitcast_fusion.5 = f32[32,256,256]{2,1,0:T(8,128)} fusion(f32[32,256,256]{1,2,0:T(8,128)} %fusion.76, f32[32,256,256]{1,2,0:T(8,128)} %fusion.79, bf16[32,128,256]{2,1,0:T(8,128)(2,1)S(1)} %bitcast.252, bf16[32,3,256,128]{3,2,0,1:T(8,128)(2,1)S(1)} %bitcast.188), kind=kOutput, calls=%fused_computation.11 | convolution fusion | flops 541065216 | bytes 29360128 | tf_op jit(solution)/shard_map/bij,bjc->bic/dot_general | solution.py:46
  214.1 6.2 %fusion.123 = (f32[32,128,256]{2,1,0:T(8,128)}, f32[32,128,256]{2,1,0:T(8,128)S(1)}) fusion(f32[32,256,256]{2,1,0:T(8,128)} %add_bitcast_fusion.5), kind=kLoop, calls=%fused_computation.191 | loop fusion | bytes 16777216 | tf_op jit(solution)/shard_map/slice | solution.py:52
  228.7 16.1 %fusion.37 = bf16[32,128,256]{2,1,0:T(8,128)(2,1)} fusion(f32[32,128,1]{2,1,0:T(8,128)} %bitcast.268, f32[32,128,255]{2,1,0:T(8,128)} %bitcast.236, f32[32,128,255]{2,1,0:T(8,128)} %bitcast.235, f32[32,128,1]{2,1,0:T(8,128)} %bitcast.267, f32[32,128,1]{2,1,0:T(8,128)} %bitcast.258, f32[32,128,255]{2,1,0:T(8,128)} %bitcast.226, ...), kind=kLoop, calls=%fused_computation.60 | loop fusion | flops 23068672 | bytes 35672320 | tf_op jit(solution)/shard_map/convert_element_type | solution.py:86
  244.8 6.3 %fusion.91 = f32[32,256,256]{1,2,0:T(8,128)} fusion(bf16[32,128,256]{2,1,0:T(8,128)(2,1)} %fusion.37, bf16[32,3,256,128]{3,2,0,1:T(8,128)(2,1)S(1)} %bitcast.201), kind=kOutput, calls=%fused_computation.142 | convolution fusion | flops 536870912 | bytes 12582912 | tf_op jit(solution)/shard_map/bij,bjc->bic/dot_general | solution.py:46
  251.2 10.8 %fusion.27 = bf16[4096,256]{1,0:T(8,128)(2,1)} fusion(f32[4096,1]{1,0:T(8,128)} %get-tuple-element.55, f32[4096,255]{1,0:T(8,128)} %get-tuple-element.57, f32[4096,255]{1,0:T(8,128)} %get-tuple-element.56, f32[4096,1]{1,0:T(8,128)} %get-tuple-element.54, f32[4096,1]{1,0:T(8,128)} %get-tuple-element.47, f32[4096,255]{1,0:T(8,128)S(1)} %copy-done.13, ...), kind=kLoop, calls=%fused_computation.47 | loop fusion | flops 17825792 | bytes 27283712 | tf_op jit(solution)/shard_map/convert_element_type | solution.py:86
  267.3 6.2 %fusion.80 = f32[32,256,256]{1,2,0:T(8,128)} fusion(bf16[32,128,256]{2,1,0:T(8,128)(2,1)} %fusion.37, bf16[32,3,256,128]{3,2,0,1:T(8,128)(2,1)S(1)} %bitcast.189), kind=kOutput, calls=%fused_computation.131 | convolution fusion | flops 536870912 | bytes 12582912 | tf_op jit(solution)/shard_map/bij,bjc->bic/dot_general | solution.py:46
  275.1 5.4 fusion.88
  281.3 8.6 %add_bitcast_fusion.2 = f32[32,256,256]{2,1,0:T(8,128)} fusion(f32[32,256,256]{1,2,0:T(8,128)} %fusion.88, f32[32,256,256]{1,2,0:T(8,128)S(1)} %bitcast.242, bf16[32,128,256]{2,1,0:T(8,128)(2,1)} %bitcast.253, bf16[32,3,256,128]{3,2,0,1:T(8,128)(2,1)S(1)} %bitcast.203), kind=kOutput, calls=%fused_computation.8 | convolution fusion | flops 541065216 | bytes 29360128 | tf_op jit(solution)/shard_map/bij,bjc->bic/dot_general | solution.py:46
  289.9 6.3 %fusion.122 = (f32[32,128,256]{2,1,0:T(8,128)}, f32[32,128,256]{2,1,0:T(8,128)S(1)}) fusion(f32[32,256,256]{2,1,0:T(8,128)} %add_bitcast_fusion.2), kind=kLoop, calls=%fused_computation.190 | loop fusion | bytes 16777216 | tf_op jit(solution)/shard_map/slice | solution.py:52
  320.4 10.3 %add_bitcast_fusion.3 = f32[32,256,256]{2,1,0:T(8,128)} fusion(f32[32,256,256]{1,2,0:T(8,128)} %fusion.77, f32[32,256,256]{1,2,0:T(8,128)} %fusion.80, bf16[32,128,256]{2,1,0:T(8,128)(2,1)S(1)} %bitcast.254, bf16[32,3,256,128]{3,2,0,1:T(8,128)(2,1)S(1)} %bitcast.191), kind=kOutput, calls=%fused_computation.9 | convolution fusion | flops 541065216 | bytes 29360128 | tf_op jit(solution)/shard_map/bij,bjc->bic/dot_general | solution.py:46
  330.7 6.2 %fusion.121 = (f32[32,128,256]{2,1,0:T(8,128)}, f32[32,128,256]{2,1,0:T(8,128)S(1)}) fusion(f32[32,256,256]{2,1,0:T(8,128)} %add_bitcast_fusion.3), kind=kLoop, calls=%fused_computation.189 | loop fusion | bytes 16777216 | tf_op jit(solution)/shard_map/slice | solution.py:52
  345.3 16.2 %fusion.58 = bf16[32,128,256]{2,1,0:T(8,128)(2,1)} fusion(f32[32,128,1]{2,1,0:T(8,128)} %bitcast.272, f32[32,128,255]{2,1,0:T(8,128)} %bitcast.240, f32[32,128,255]{2,1,0:T(8,128)} %bitcast.239, f32[32,128,1]{2,1,0:T(8,128)} %bitcast.271, f32[32,128,1]{2,1,0:T(8,128)} %bitcast.262, f32[32,128,255]{2,1,0:T(8,128)} %bitcast.230, ...), kind=kLoop, calls=%fused_computation.87 | loop fusion | flops 23068672 | bytes 35672320 | tf_op jit(solution)/shard_map/convert_element_type | solution.py:86
  361.5 6.3 %fusion.92 = f32[32,256,256]{1,2,0:T(8,128)} fusion(bf16[32,128,256]{2,1,0:T(8,128)(2,1)} %fusion.58, bf16[32,3,256,128]{3,2,0,1:T(8,128)(2,1)S(1)} %bitcast.204), kind=kOutput, calls=%fused_computation.143 | convolution fusion | flops 536870912 | bytes 12582912 | tf_op jit(solution)/shard_map/bij,bjc->bic/dot_general | solution.py:46
  367.9 11.0 %fusion.48 = bf16[4096,256]{1,0:T(8,128)(2,1)} fusion(f32[4096,1]{1,0:T(8,128)} %get-tuple-element.43, f32[4096,255]{1,0:T(8,128)} %get-tuple-element.45, f32[4096,255]{1,0:T(8,128)} %get-tuple-element.44, f32[4096,1]{1,0:T(8,128)} %get-tuple-element.42, f32[4096,1]{1,0:T(8,128)} %get-tuple-element.35, f32[4096,255]{1,0:T(8,128)S(1)} %copy-done.20, ...), kind=kLoop, calls=%fused_computation.74 | loop fusion | flops 17825792 | bytes 27283712 | tf_op jit(solution)/shard_map/convert_element_type | solution.py:86
  393.2 10.9 %add_bitcast_fusion = f32[32,256,256]{2,1,0:T(8,128)} fusion(f32[32,256,256]{1,2,0:T(8,128)} %fusion.89, f32[32,256,256]{1,2,0:T(8,128)} %fusion.92, bf16[32,128,256]{2,1,0:T(8,128)(2,1)} %bitcast.247, bf16[32,3,256,128]{3,2,0,1:T(8,128)(2,1)S(1)} %bitcast.206), kind=kOutput, calls=%fused_computation.6 | convolution fusion | flops 541065216 | bytes 29360128 | tf_op jit(solution)/shard_map/bij,bjc->bic/dot_general | solution.py:46
  404.2 6.2 %fusion.120 = (f32[32,128,256]{2,1,0:T(8,128)}, f32[32,128,256]{2,1,0:T(8,128)S(1)}) fusion(f32[32,256,256]{2,1,0:T(8,128)} %add_bitcast_fusion), kind=kLoop, calls=%fused_computation.188 | loop fusion | bytes 16777216 | tf_op jit(solution)/shard_map/slice | solution.py:52
  434.6 8.0 %add_bitcast_fusion.1 = f32[32,256,256]{2,1,0:T(8,128)} fusion(f32[32,256,256]{1,2,0:T(8,128)} %fusion.78, f32[32,256,256]{1,2,0:T(8,128)S(1)} %fusion.81, bf16[32,128,256]{2,1,0:T(8,128)(2,1)S(1)} %bitcast.248, bf16[32,3,256,128]{3,2,0,1:T(8,128)(2,1)S(1)} %bitcast.194), kind=kOutput, calls=%fused_computation.7 | convolution fusion | flops 541065216 | bytes 29360128 | tf_op jit(solution)/shard_map/bij,bjc->bic/dot_general | solution.py:46
  455.0 7.7 %fusion.69 = bf16[4096,256]{1,0:T(8,128)(2,1)S(1)} fusion(f32[4096,1]{1,0:T(8,128)} %get-tuple-element.31, f32[4096,255]{1,0:T(8,128)} %get-tuple-element.33, f32[4096,255]{1,0:T(8,128)S(1)} %get-tuple-element.32, f32[4096,1]{1,0:T(8,128)} %get-tuple-element.30, f32[4096,1]{1,0:T(8,128)} %get-tuple-element.23, f32[4096,255]{1,0:T(8,128)S(1)} %copy-done.42, ...), kind=kLoop, calls=%fused_computation.101 | loop fusion | flops 17825792 | bytes 27283712 | tf_op jit(solution)/shard_map/convert_element_type | solution.py:86
  465.1 10.7 %reduce-scatter.2.cloned.1.call-done = bf16[256,256]{1,0:T(8,128)(2,1)} async-done(((bf16[512,256]{1,0:T(8,128)(2,1)}), bf16[256,256]{1,0:T(8,128)(2,1)}) %reduce-scatter.2.cloned.1.call-update) | async-done | bytes 131088 | tf_op jit(solution)/shard_map/reduce_scatter | solution.py:94
  481.2 8.7 %copy.16 = bf16[2048,2,128]{2,1,0:T(2,128)(2,1)S(1)} copy(bf16[2048,2,128]{2,0,1:T(8,128)(2,1)S(1)} %pad_maximum_fusion.8) | data formatting | bytes 2097152 | tf_op jit(solution)/shard_map/stack | solution.py:60
  489.9 54.5 %all-gather.2.cloned.1.call-done = bf16[256,4096]{1,0:T(8,128)(2,1)} async-done(((bf16[256,256]{1,0:T(8,128)(2,1)}), bf16[256,4096]{1,0:T(8,128)(2,1)}) %all-gather.2.cloned.1.call-update) | async-done | bytes 2097168 | tf_op jit(solution)/shard_map/all_gather | solution.py:103
  (217 shorter events, 216.5 us)
Async XLA Ops:
  6.5 31.3 %copy-start = (f32[256]{0:T(256)S(1)}, f32[256]{0:T(256)}, u32[]{:S(2)}) copy-start(f32[256]{0:T(256)} %param.12) | copy-start | bytes 3076
  6.5 469.2 %reduce-scatter.2.cloned.1.call-start = ((), (), s32[]{:S(2)}) async-start(), calls=%async_computation.1 | async-start | bytes 393216 | tf_op jit(solution)/shard_map/reduce_scatter | solution.py:94
  7.4 38.4 %collective-permute-start = (bf16[128,256]{1,0:T(8,128)(2,1)S(1)}, bf16[128,256]{1,0:T(8,128)(2,1)S(1)}, u32[]{:S(2)}, u32[]{:S(2)}) collective-permute-start(bf16[128,256]{1,0:T(8,128)(2,1)S(1)} %get-tuple-element.85), channel_id=1, source_target_pairs={{0,1},{2,3},{4,5},{6,7},{8,9},{10,11},{12,13},{14,15},{16,17},{18,... | collective-permute-start | bytes 196616 | tf_op jit(solution)/shard_map/ppermute | solution.py:20
  9.8 36.0 %collective-permute-start.1 = (bf16[128,256]{1,0:T(8,128)(2,1)S(1)}, bf16[128,256]{1,0:T(8,128)(2,1)S(1)}, u32[]{:S(2)}, u32[]{:S(2)}) collective-permute-start(bf16[128,256]{1,0:T(8,128)(2,1)S(1)} %get-tuple-element.84), channel_id=1, source_target_pairs={{1,0},{3,2},{5,4},{7,6},{9,8},{11,10},{13,12},{15,14},{17,16},{19,... | collective-permute-start | bytes 196616 | tf_op jit(solution)/shard_map/ppermute | solution.py:22
  20.9 7.0 %copy-start.3 = (bf16[32,128,3,2,128]{4,1,3,0,2:T(8,128)(2,1)}, bf16[32,128,3,2,128]{4,1,3,0,2:T(8,128)(2,1)S(1)}, u32[]{:S(2)}) copy-start(bf16[32,128,3,2,128]{4,1,3,0,2:T(8,128)(2,1)S(1)} %copy.15) | copy-start | bytes 18874372
  20.9 7.0 %copy-start.21 = (bf16[4096,256]{1,0:T(8,128)(2,1)S(1)}, bf16[4096,256]{1,0:T(8,128)(2,1)}, u32[]{:S(2)}) copy-start(bf16[4096,256]{1,0:T(8,128)(2,1)} %param.9) | copy-start | bytes 6291460
  33.2 12.0 %copy-start.55 = (s32[512]{0:T(512)S(1)}, s32[512]{0:T(512)}, u32[]{:S(2)}) copy-start(s32[512]{0:T(512)} %param.14) | copy-start | bytes 6148
  65.7 6.4 %copy-start.43 = (f32[32,128,256]{2,1,0:T(8,128)S(1)}, f32[32,128,256]{2,1,0:T(8,128)}, u32[]{:S(2)}) copy-start(f32[32,128,256]{2,1,0:T(8,128)} %get-tuple-element.20) | copy-start | bytes 12582916
  72.0 10.0 %slice-start = ((s8[6291456]{0:T(1024)(128)(4,1)}), s8[4194304]{0:T(1024)(128)(4,1)S(1)}, s32[]{:S(2)}) async-start(s8[6291456]{0:T(1024)(128)(4,1)} %bitcast.182), calls=%async_computation.3 | async-start | bytes 8388608
  74.8 7.3 %slice-start.1 = ((s8[6291456]{0:T(1024)(128)(4,1)}), s8[2097152]{0:T(1024)(128)(4,1)S(1)}, s32[]{:S(2)}) async-start(s8[6291456]{0:T(1024)(128)(4,1)} %bitcast.182), calls=%async_computation.4 | async-start | bytes 4194304
  128.1 6.3 %copy-start.17 = (f32[4096,255]{1,0:T(8,128)S(1)}, f32[4096,255]{1,0:T(8,128)}, u32[]{:S(2)}) copy-start(f32[4096,255]{1,0:T(8,128)} %get-tuple-element.60) | copy-start | bytes 12533764
  128.1 6.3 %copy-start.18 = (f32[4096,255]{1,0:T(8,128)S(1)}, f32[4096,255]{1,0:T(8,128)}, u32[]{:S(2)}) copy-start(f32[4096,255]{1,0:T(8,128)} %get-tuple-element.61) | copy-start | bytes 12533764
  145.9 10.7 %collective-permute-start.2 = (bf16[128,256]{1,0:T(8,128)(2,1)S(1)}, bf16[128,256]{1,0:T(8,128)(2,1)S(1)}, u32[]{:S(2)}, u32[]{:S(2)}) collective-permute-start(bf16[128,256]{1,0:T(8,128)(2,1)S(1)} %get-tuple-element.81), channel_id=1, source_target_pairs={{0,1},{2,3},{4,5},{6,7},{8,9},{10,11},{12,13},{14,15},{16,17},{18,... | collective-permute-start | bytes 196616 | tf_op jit(solution)/shard_map/ppermute | solution.py:20
  149.0 7.6 %copy-start.46 = (bf16[4096,256]{1,0:T(8,128)(2,1)S(1)}, bf16[4096,256]{1,0:T(8,128)(2,1)}, u32[]{:S(2)}) copy-start(bf16[4096,256]{1,0:T(8,128)(2,1)} %fusion.6) | copy-start | bytes 6291460
  149.0 7.6 %collective-permute-start.3 = (bf16[128,256]{1,0:T(8,128)(2,1)S(1)}, bf16[128,256]{1,0:T(8,128)(2,1)S(1)}, u32[]{:S(2)}, u32[]{:S(2)}) collective-permute-start(bf16[128,256]{1,0:T(8,128)(2,1)S(1)} %get-tuple-element.80), channel_id=1, source_target_pairs={{1,0},{3,2},{5,4},{7,6},{9,8},{11,10},{13,12},{15,14},{17,16},{19,... | collective-permute-start | bytes 196616 | tf_op jit(solution)/shard_map/ppermute | solution.py:22
  156.6 7.0 %slice-start.4 = ((s8[8388608]{0:T(1024)(128)(4,1)}), s8[4194304]{0:T(1024)(128)(4,1)S(1)}, s32[]{:S(2)}) async-start(s8[8388608]{0:T(1024)(128)(4,1)} %bitcast.243), calls=%async_computation.7 | async-start | bytes 8388608
  244.8 6.3 %copy-start.12 = (f32[4096,255]{1,0:T(8,128)S(1)}, f32[4096,255]{1,0:T(8,128)}, u32[]{:S(2)}) copy-start(f32[4096,255]{1,0:T(8,128)} %get-tuple-element.48) | copy-start | bytes 12533764
  244.8 6.3 %copy-start.13 = (f32[4096,255]{1,0:T(8,128)S(1)}, f32[4096,255]{1,0:T(8,128)}, u32[]{:S(2)}) copy-start(f32[4096,255]{1,0:T(8,128)} %get-tuple-element.49) | copy-start | bytes 12533764
  244.8 6.3 %copy-start.52 = (f32[4096]{0:T(1024)S(1)}, f32[4096]{0:T(1024)}, u32[]{:S(2)}) copy-start(f32[4096]{0:T(1024)} %get-tuple-element.98) | copy-start | bytes 49156
  262.8 10.7 %collective-permute-start.4 = (bf16[128,256]{1,0:T(8,128)(2,1)S(1)}, bf16[128,256]{1,0:T(8,128)(2,1)S(1)}, u32[]{:S(2)}, u32[]{:S(2)}) collective-permute-start(bf16[128,256]{1,0:T(8,128)(2,1)S(1)} %get-tuple-element.77), channel_id=1, source_target_pairs={{0,1},{2,3},{4,5},{6,7},{8,9},{10,11},{12,13},{14,15},{16,17},{18,... | collective-permute-start | bytes 196616 | tf_op jit(solution)/shard_map/ppermute | solution.py:20
  265.9 7.6 %copy-start.47 = (bf16[4096,256]{1,0:T(8,128)(2,1)S(1)}, bf16[4096,256]{1,0:T(8,128)(2,1)}, u32[]{:S(2)}) copy-start(bf16[4096,256]{1,0:T(8,128)(2,1)} %fusion.27) | copy-start | bytes 6291460
  265.9 7.6 %collective-permute-start.5 = (bf16[128,256]{1,0:T(8,128)(2,1)S(1)}, bf16[128,256]{1,0:T(8,128)(2,1)S(1)}, u32[]{:S(2)}, u32[]{:S(2)}) collective-permute-start(bf16[128,256]{1,0:T(8,128)(2,1)S(1)} %get-tuple-element.76), channel_id=1, source_target_pairs={{1,0},{3,2},{5,4},{7,6},{9,8},{11,10},{13,12},{15,14},{17,16},{19,... | collective-permute-start | bytes 196616 | tf_op jit(solution)/shard_map/ppermute | solution.py:22
  273.5 7.0 %slice-start.2 = ((s8[8388608]{0:T(1024)(128)(4,1)}), s8[4194304]{0:T(1024)(128)(4,1)S(1)}, s32[]{:S(2)}) async-start(s8[8388608]{0:T(1024)(128)(4,1)} %bitcast.241), calls=%async_computation.5 | async-start | bytes 8388608
  361.5 6.4 %copy-start.19 = (f32[4096,255]{1,0:T(8,128)S(1)}, f32[4096,255]{1,0:T(8,128)}, u32[]{:S(2)}) copy-start(f32[4096,255]{1,0:T(8,128)} %get-tuple-element.36) | copy-start | bytes 12533764
  361.5 6.4 %copy-start.20 = (f32[4096,255]{1,0:T(8,128)S(1)}, f32[4096,255]{1,0:T(8,128)}, u32[]{:S(2)}) copy-start(f32[4096,255]{1,0:T(8,128)} %get-tuple-element.37) | copy-start | bytes 12533764
  361.5 6.4 %copy-start.50 = (f32[4096]{0:T(1024)S(1)}, f32[4096]{0:T(1024)}, u32[]{:S(2)}) copy-start(f32[4096]{0:T(1024)} %get-tuple-element.97) | copy-start | bytes 49156
  379.7 7.3 %collective-permute-start.6 = (bf16[128,256]{1,0:T(8,128)(2,1)S(1)}, bf16[128,256]{1,0:T(8,128)(2,1)S(1)}, u32[]{:S(2)}, u32[]{:S(2)}) collective-permute-start(bf16[128,256]{1,0:T(8,128)(2,1)S(1)} %get-tuple-element.73), channel_id=1, source_target_pairs={{0,1},{2,3},{4,5},{6,7},{8,9},{10,11},{12,13},{14,15},{16,17},{18,... | collective-permute-start | bytes 196616 | tf_op jit(solution)/shard_map/ppermute | solution.py:20
  382.8 4.3 collective-permute-start.7
  455.0 7.7 %copy-start.56 = (s32[512]{0:T(512)S(1)}, s32[512]{0:T(512)}, u32[]{:S(2)}) copy-start(s32[512]{0:T(512)} %broadcast_subtract_fusion) | copy-start | bytes 6148
  462.7 13.1 %copy-start.54 = (f32[2048]{0:T(1024)S(1)}, f32[2048]{0:T(1024)}, u32[]{:S(2)}) copy-start(f32[2048]{0:T(1024)} %param.13) | copy-start | bytes 24580
  465.0 79.3 %all-gather.2.cloned.1.call-start = ((), (), s32[]{:S(2)}) async-start(), calls=%async_computation.2 | async-start | bytes 2228224 | tf_op jit(solution)/shard_map/all_gather | solution.py:103
  475.8 71.6 %copy-start.1 = (f32[256]{0:T(256)S(1)}, f32[256]{0:T(256)}, u32[]{:S(2)}) copy-start(f32[256]{0:T(256)} %param.12) | copy-start | bytes 3076
  (41 other events, 161.4 us)
Sparse Core Ops, SparseCore 0:
  465.1 10.5 reduce-scatter.1
  478.5 65.8 all-gather.1
where the time goes:
time: 564 us; the launch traced here: 554 us
  local copies, waits for them, and re-layouts  174 us (31%)
  matrix products  162 us (29%)
  other arithmetic  121 us (21%)
  waiting for transfers between devices  65.2 us (12%)
  starting transfers between devices  17.1 us (3%)
  between operations  14.3 us (3%)
    dot_general x24, matrix products, apply_blocks(): jnp.einsum('bij,bjc->bic', ordered[:, offset], stacked[offset:offset + bl...  157 us
    convert_element_type x7, other arithmetic, local(): columns = (damping[:, None] * combined).astype(jnp.bfloat16)  88.6 us
    slice x24, local copies, waits for them, and re-layouts, times_unit(): lower = jnp.roll(values, 1, axis=1)  75.3 us
    all_gather x1, waiting for transfers between devices, local(): lax.all_gather(owned, 'freq', axis=1, tiled=True)  54.5 us
    slice x8, local copies, waits for them, and re-layouts, apply_blocks(): real_part = product[:, :block_size].reshape(block_count * block_size, width)  44.6 us
    unnamed x126, local copies, waits for them, and re-layouts  25.2 us
    add x4, other arithmetic, apply_blocks(): return real_part + times_unit(imag_part)  14.6 us
    reshape x2, local copies, waits for them, and re-layouts, order_blocks(): shaped = blocks.reshape(block_count, block_size, 3, 2, block_size)  11.6 us
  transfers between devices with their start and end apart: 10, of which 2 were waited for; matrix products, arithmetic and copies ran while one was open for 11% of the time, Pallas kernels for 0%

commit v1 on v0

v1 whole, which is shorter than its diff:
```python
import functools
import math

import jax
import jax.numpy as jnp
from jax import lax
from jax.experimental import pallas as pl
from jax.experimental.pallas import tpu as pltpu
from jax.sharding import PartitionSpec as P

NT = 2048
STEPS = 4

COS_TERMS = (1.0, -19.739208221435547, 64.93939208984375, -85.45665740966797,
             60.242130279541016, -26.4046688079834, 7.800131320953369, -1.453112244606018)
SIN_TERMS = (6.2831854820251465, -41.34170150756836, 81.6052474975586, -76.70580291748047,
             42.05775451660156, -15.086565017700195, 3.7813189029693604, -0.6207787394523621)

MESH = pl.DeviceIdType.MESH
F32 = jnp.float32
BF16 = jnp.bfloat16


def poly(terms, z):
    total = jnp.full_like(z, terms[-1])
    for term in terms[-2::-1]:
        total = total * z + F32(term)
    return total


def unroll_of(count, choices=(5, 4, 3, 2, 1)):
    return next(c for c in choices if count % c == 0)


def split_rows(rows, parts):
    unit = 16
    units = rows // unit
    cuts = [round(units * i / parts) * unit for i in range(parts)] + [rows]
    return [(cuts[i], cuts[i + 1] - cuts[i]) for i in range(parts)]


def plan_of(rows, bits):
    parts = min(3, max(1, bits - 1))
    plan = []
    for i, (start, count) in enumerate(split_rows(rows, parts)):
        low = list(range(bits - 1))
        order = low[i:] + low[:i] + [bits - 1]
        plan.append((start, count, order))
    return plan


def kernel(depth_n, freq_n, bits, factor, plan,
           field, main_hbm, side_hbm, weights, freqs, receivers, floors, out,
           raw_main, raw_side, spread, ops, w_buf, final, halo, picked, owned, pick_in,
           basis, sums, *rest):
    n_parts = len(plan)
    send_bufs = rest[:n_parts]
    recv_bufs = rest[n_parts:2 * n_parts]
    load_sem, halo_send, halo_recv, pick_send, pick_recv, rs_send, rs_recv = rest[2 * n_parts:]
    rows, width = field.shape
    half = width // 2
    bs = raw_main.shape[1]
    kc = 6
    nb = rows // bs
    bw = 2 * bs
    me_d = lax.axis_index("depth")
    me_f = lax.axis_index("freq")
    first_row = me_d * rows

    for which, (src, dst) in enumerate(((main_hbm, raw_main), (side_hbm, raw_side))):
        def start(b, carry, src=src, dst=dst, which=which):
            at = pl.ds(pl.multiple_of(b * kc * bs, kc * bs), kc * bs)
            pltpu.make_async_copy(src.at[at], dst.at[at], load_sem.at[which, b]).start()
            return carry
        lax.fori_loop(0, nb, start, 0)

    barrier = pltpu.get_barrier_semaphore()
    for off in range(1, depth_n):
        pl.semaphore_signal(barrier, inc=1, device_id={"depth": lax.rem(me_d + off, depth_n)},
                            device_id_type=MESH)
    partners = []
    for j in range(bits):
        mine = lax.rem(me_f // (1 << j), 2)
        partners.append((mine, me_f + (1 - 2 * mine) * (1 << j)))
        pl.semaphore_signal(barrier, inc=1, device_id={"freq": partners[j][1]}, device_id_type=MESH)

    def put_w(parity, b, re, im):
        base = pl.multiple_of((b + 1) * bw, bw)
        top, low = pl.ds(base, bs), pl.ds(pl.multiple_of(base + bs, bs), bs)
        w_buf[parity, top, :half] = re
        w_buf[parity, top, half:] = im
        w_buf[parity, low, :half] = -im
        w_buf[parity, low, half:] = re

    from_col = lax.broadcasted_iota(jnp.int32, (width, width), 0)
    to_col = lax.broadcasted_iota(jnp.int32, (width, width), 1)
    wanted = jnp.where(to_col < half, 2 * to_col, 2 * (to_col - half) + 1)
    order = jnp.where(from_col == wanted, 1.0, 0.0).astype(BF16)

    def enter(b, carry):
        at = pl.ds(pl.multiple_of(b * bs, bs), bs)
        got = jnp.dot(field[at, :], order, preferred_element_type=F32).astype(BF16)
        put_w(0, b, got[:, :half], got[:, half:])
        return carry

    enter(0, 0)
    enter(nb - 1, 0)
    lax.fori_loop(1, nb - 1, enter, 0, unroll=2)
    zero_edge = jnp.zeros((bw, width), BF16)
    for parity in range(2):
        w_buf[parity, :bw, :] = zero_edge
        w_buf[parity, (nb + 1) * bw:, :] = zero_edge

    pl.semaphore_wait(barrier, depth_n - 1 + bits)

    def halo_copy(step, side):
        edge = (1 if side == 0 else nb) * bw
        to = lax.rem(me_d + (depth_n - 1 if side == 0 else 1), depth_n)
        return pltpu.make_async_remote_copy(
            src_ref=w_buf.at[step % 2, pl.ds(edge, bw)],
            dst_ref=halo.at[step, side],
            send_sem=halo_send.at[step, side],
            recv_sem=halo_recv.at[step, side],
            device_id={"depth": to},
            device_id_type=MESH,
        )

    has_above = me_d > 0
    has_below = me_d < depth_n - 1

    def halo_start(step):
        if depth_n == 1:
            return

        @pl.when(has_above)
        def _():
            halo_copy(step, 0).start()

        @pl.when(has_below)
        def _():
            halo_copy(step, 1).start()

    def halo_finish(step):
        if depth_n == 1:
            return

        @pl.when(has_above)
        def _():
            halo_copy(step, 0).wait_send()
            halo_copy(step, 1).wait_recv()
            w_buf[step % 2, :bw, :] = halo[step, 1]

        @pl.when(has_below)
        def _():
            halo_copy(step, 1).wait_send()
            halo_copy(step, 0).wait_recv()
            w_buf[step % 2, (nb + 1) * bw:, :] = halo[step, 0]

    halo_start(0)

    times = out.shape[1]
    lane = lax.broadcasted_iota(jnp.int32, (half, times), 1)

    def basis_of(c, carry):
        n = (c * times + lane).astype(F32)
        y = (freqs[...] * n) * F32(1.0 / NT)
        p = y - jnp.floor(y)
        r = jnp.where(p > 0.5, p - 1.0, p)
        z = r * r
        basis[c, :half, :] = poly(COS_TERMS, z).astype(BF16)
        basis[c, half:, :] = (-(r * poly(SIN_TERMS, z))).astype(BF16)
        return carry

    lax.fori_loop(0, freq_n, basis_of, 0)

    wr = weights[0:1, :]
    wi = weights[1:2, :]
    row_iota = lax.broadcasted_iota(jnp.int32, (bs, half), 0)

    def multiply(step, b):
        parity = step % 2
        near = pl.ds(pl.multiple_of(b * bw, bw), 3 * bw)
        acc = jnp.dot(ops[b], w_buf[parity, near, :], preferred_element_type=F32)
        m, c = acc[:bs], acc[bs:]
        re = m[:, :half] + wr * c[:, :half] - wi * c[:, half:]
        im = m[:, half:] + wr * c[:, half:] + wi * c[:, :half]
        damp = jnp.where(row_iota + (first_row + b * bs) >= floors[step], F32(0.5), F32(1.0))
        re = (damp * re).astype(BF16)
        im = (damp * im).astype(BF16)
        if step == STEPS - 1:
            at = pl.ds(pl.multiple_of(b * bs, bs), bs)
            final[at, :half] = re
            final[at, half:] = im
        else:
            put_w(1 - parity, b, re, im)

    def prepare(b):
        at = pl.ds(pl.multiple_of(b * kc * bs, kc * bs), kc * bs)
        for which, (src, dst) in enumerate(((main_hbm, raw_main), (side_hbm, raw_side))):
            pltpu.make_async_copy(src.at[at], dst.at[at], load_sem.at[which, b]).wait()
            spread[which] = dst[at, :].astype(F32)
            for piece in range(kc):
                ops[b, which * bs:(which + 1) * bs, piece * bs:(piece + 1) * bs] = spread[
                    which, pl.ds(piece, bs, stride=kc), :].astype(BF16)

    prepare(0)
    prepare(nb - 1)
    prepare(1)

    def first_step(b, carry):
        multiply(0, b)

        @pl.when(b + 1 < nb - 1)
        def _():
            prepare(b + 1)

        return carry

    lax.fori_loop(1, nb - 1, first_step, 0)
    halo_finish(0)
    multiply(0, 0)
    multiply(0, nb - 1)
    for step in range(1, STEPS):
        multiply(step, 1)
        multiply(step, 2)
        halo_start(step)

        def inner(b, carry, step=step):
            multiply(step, b)
            return carry

        lax.fori_loop(3, nb - 1, inner, 0, unroll=unroll_of(nb - 4))
        halo_finish(step)
        multiply(step, 0)
        multiply(step, nb - 1)

    here = out.shape[0]
    chunk = min(rows, 1024)

    def pick(owner):
        at = pl.ds(pl.multiple_of(owner * here, here), here)
        local = receivers[at, :] - first_row
        total = jnp.zeros((here, width), F32)
        for base in range(0, rows, chunk):
            marks = [
                jnp.where(local == lax.broadcasted_iota(jnp.int32, local.shape, 1) + (base + sub),
                          1.0, 0.0).astype(BF16)
                for sub in range(0, chunk, local.shape[1])
            ]
            total = total + jnp.dot(jnp.concatenate(marks, axis=1), final[base:base + chunk, :],
                                    preferred_element_type=F32)
        return total

    def pick_copy(off):
        return pltpu.make_async_remote_copy(
            src_ref=picked.at[off - 1],
            dst_ref=pick_in.at[off - 1],
            send_sem=pick_send.at[off - 1],
            recv_sem=pick_recv.at[off - 1],
            device_id={"depth": lax.rem(me_d + off, depth_n)},
            device_id_type=MESH,
        )

    for off in range(1, depth_n):
        picked[off - 1] = pick(lax.rem(me_d + off, depth_n)).astype(BF16)
    for off in range(1, depth_n):
        pick_copy(off).start()
    mine_rows = pick(me_d)
    for off in range(1, depth_n):
        pick_copy(off).wait()
        mine_rows = mine_rows + pick_in[off - 1].astype(F32)
    owned[...] = mine_rows.astype(BF16)

    def chunk_at(part_order, q):
        c = 0
        for t, j in enumerate(part_order):
            c = c + lax.rem(q // (1 << (bits - 1 - t)), 2) * (1 << j)
        return c

    def partial(part, q):
        start, count, part_order = plan[part]
        return jnp.dot(owned[start:start + count, :], basis[chunk_at(part_order, q)],
                       preferred_element_type=F32)

    def offset_of(stage):
        return freq_n - (freq_n >> stage)

    def rs_copy(part, stage):
        size = freq_n >> (stage + 1)
        at = pl.ds(offset_of(stage), size)
        j = plan[part][2][stage]
        return pltpu.make_async_remote_copy(
            src_ref=send_bufs[part].at[at],
            dst_ref=recv_bufs[part].at[at],
            send_sem=rs_send.at[part, stage],
            recv_sem=rs_recv.at[part, stage],
            device_id={"freq": partners[j][1]},
            device_id_type=MESH,
        )

    if bits == 0:
        out[...] = jnp.dot(owned[...], basis[0], preferred_element_type=F32) * factor
        return

    def sweep(size, body):
        def one(q, carry):
            body(q)
            return carry
        lax.fori_loop(0, size, one, 0, unroll=min(2, size))

    size = freq_n // 2
    for part in range(n_parts):
        mine = partners[plan[part][2][0]][0]

        def fill(q, part=part, mine=mine):
            send_bufs[part][q] = partial(part, (1 - mine) * size + q).astype(BF16)

        sweep(size, fill)
    for part in range(n_parts):
        rs_copy(part, 0).start()
    for part in range(n_parts):
        start, count, _ = plan[part]
        mine = partners[plan[part][2][0]][0]

        def keep(q, part=part, mine=mine, start=start, count=count):
            sums[q, start:start + count, :] = partial(part, mine * size + q)

        sweep(size, keep)
    for stage in range(bits):
        size = freq_n >> (stage + 1)
        base = offset_of(stage)
        last = stage == bits - 1
        for part in range(n_parts):
            start, count, part_order = plan[part]
            rs_copy(part, stage).wait()
            at = slice(start, start + count)
            if last:
                out[at, :] = (sums[0, at, :] + recv_bufs[part][base].astype(F32)) * factor
                continue
            nxt = size // 2
            mine = partners[part_order[stage + 1]][0]
            into = offset_of(stage + 1)

            def send(q, part=part, at=at, mine=mine, nxt=nxt, base=base, into=into):
                k = (1 - mine) * nxt + q
                send_bufs[part][into + q] = (
                    sums[k, at, :] + recv_bufs[part][base + k].astype(F32)).astype(BF16)

            sweep(nxt, send)
            rs_copy(part, stage + 1).start()

            def hold(q, part=part, at=at, mine=mine, nxt=nxt, base=base):
                k = mine * nxt + q
                sums[q, at, :] = sums[k, at, :] + recv_bufs[part][base + k].astype(F32)

            sweep(nxt, hold)


def local(depth_n, freq_n, pressure_field, block_main, block_coupled, coupling, frequencies,
          receivers, floors):
    rows, width = pressure_field.shape
    bs = block_main.shape[3]
    half = width // 2
    nb = rows // bs
    bits = freq_n.bit_length() - 1
    here = receivers.shape[0] // depth_n
    times = NT // freq_n
    factor = 1.0 / math.sqrt(frequencies.shape[0])
    plan = plan_of(here, bits)
    weights = coupling.reshape(half, 2).T
    own = lax.dynamic_slice_in_dim(frequencies, lax.axis_index("freq") * half, half)
    freqs = jnp.broadcast_to(own[:, None], (half, times))
    spots = jnp.broadcast_to(receivers[:, None], (receivers.shape[0], bs))
    vmem = pl.BlockSpec(memory_space=pltpu.VMEM)
    hbm = pl.BlockSpec(memory_space=pl.ANY)
    away = max(depth_n - 1, 1)
    slots = max(freq_n - 1, 1)
    return pl.pallas_call(
        functools.partial(kernel, depth_n, freq_n, bits, factor, plan),
        out_shape=jax.ShapeDtypeStruct((here, times), F32),
        in_specs=[vmem, hbm, hbm, vmem, vmem, vmem, pl.BlockSpec(memory_space=pltpu.SMEM)],
        out_specs=vmem,
        scratch_shapes=[
            pltpu.VMEM((rows * 6, bs), BF16),
            pltpu.VMEM((rows * 6, bs), BF16),
            pltpu.VMEM((2, 6 * bs, bs), F32),
            pltpu.VMEM((nb, 2 * bs, 6 * bs), BF16),
            pltpu.VMEM((2, (nb + 2) * 2 * bs, width), BF16),
            pltpu.VMEM((rows, width), BF16),
            pltpu.VMEM((STEPS, 2, 2 * bs, width), BF16),
            pltpu.VMEM((away, here, width), BF16),
            pltpu.VMEM((here, width), BF16),
            pltpu.VMEM((away, here, width), BF16),
            pltpu.VMEM((freq_n, width, times), BF16),
            pltpu.VMEM((max(freq_n // 2, 1), here, times), F32),
            *[pltpu.VMEM((slots, count, times), BF16) for _, count, _ in plan],
            *[pltpu.VMEM((slots, count, times), BF16) for _, count, _ in plan],
            pltpu.SemaphoreType.DMA((2, nb)),
            pltpu.SemaphoreType.DMA((STEPS, 2)),
            pltpu.SemaphoreType.DMA((STEPS, 2)),
            pltpu.SemaphoreType.DMA((away,)),
            pltpu.SemaphoreType.DMA((away,)),
            pltpu.SemaphoreType.DMA((len(plan), max(bits, 1))),
            pltpu.SemaphoreType.DMA((len(plan), max(bits, 1))),
        ],
        compiler_params=pltpu.CompilerParams(
            collective_id=0, has_side_effects=True, vmem_limit_bytes=64 * 1024 * 1024 - 128 * 1024
        ),
    )(
        pressure_field,
        block_main.reshape(rows * 6, bs),
        block_coupled.reshape(rows * 6, bs),
        weights,
        freqs,
        spots,
        floors,
    )


def solution(mesh):
    in_specs = (
        P("depth", "freq"),
        P("depth", None, None, None),
        P("depth", None, None, None),
        P("freq"),
        P(),
        P(),
        P(),
    )
    body = functools.partial(local, mesh.shape["depth"], mesh.shape["freq"])
    return jax.shard_map(body, mesh=mesh, in_specs=in_specs, out_specs=P("depth", "freq"),
                         check_vma=False)
```

time: 564 us -> 80.9 us (0.14); the launches traced: 554 us -> 80.7 us
  local copies, waits for them, and re-layouts: 174 us -> 6.01 us
  matrix products: 162 us -> 0 us
  other arithmetic: 121 us -> 0 us
  Pallas kernels: 0 us -> 74.6 us
  waiting for transfers between devices: 65.2 us -> 0 us
  starting transfers between devices: 17.1 us -> 0 us
  between operations: 14.3 us -> 0.02 us
    dot_general x26 -> x0, matrix products: 162 us -> none  [the longest x24 157 us: apply_blocks(): jnp.einsum('bij,bjc->bic', ordered[:, offset], stacked[offset:offset + bl...]
    slice x37 -> x0, local copies, waits for them, and re-layouts: 125 us -> none  [the longest x24 75.3 us: times_unit(): lower = jnp.roll(values, 1, axis=1)]
    convert_element_type x8 -> x0, other arithmetic: 88.6 us -> none  [the longest x7 88.6 us: local(): columns = (damping[:, None] * combined).astype(jnp.bfloat16)]
    pallas_call x0 -> x1, Pallas kernels: none -> 74.6 us  [local(): pl.pallas_call(functools.partial(kernel, depth_n, freq_n, bits, factor, p...]
    all_gather x1 -> x0, waiting for transfers between devices: 54.5 us -> none  [local(): lax.all_gather(owned, 'freq', axis=1, tiled=True)]
    unnamed x126 -> x1, local copies, waits for them, and re-layouts: 25.2 us -> 1.57 us
    ppermute x8 -> x0, starting transfers between devices: 17.1 us -> none  [the longest x4 11.5 us: padded_2(): lax.ppermute(tail, axis, [(i, (i + 1) % count) for i in range(ends)])]
    add x4 -> x0, other arithmetic: 14.6 us -> none  [apply_blocks(): return real_part + times_unit(imag_part)]
  transfers between devices with their start and end apart: 10 -> 0, of which waited for: 2 -> 0; matrix products, arithmetic and copies ran while one was open for 11% -> 0% of each run, Pallas kernels for 0% -> 0%
where the time goes in v1:
time: 80.9 us; the launch traced here: 80.7 us
  Pallas kernels  74.6 us (92%)
  local copies, waits for them, and re-layouts  6.01 us (7%)
    pallas_call x1, Pallas kernels, local(): pl.pallas_call(functools.partial(kernel, depth_n, freq_n, bits, factor, p...  74.6 us

profile of v1, /device:TPU:0, one launch (start us, length us, event | category | flops | bytes accessed | tf_op | source)
XLA Modules:
  0.0 80.7 jit_solution(9868295797870986959)
XLA Ops:
  0.0 0.8 dynamic_slice.3
  0.8 0.7 broadcast_in_dim.4.freqs
  1.5 0.8 %reshape.13 = f32[128,2]{1,0:T(8,128)S(1)} reshape(f32[256]{0:T(256)} %param.10) | data formatting | bytes 2048 | tf_op jit(solution)/shard_map/reshape | solution.py:370
  2.3 0.6 copy.8
  2.9 1.5 %broadcast_in_dim.5.receivers = s32[512,128]{1,0:T(8,128)} broadcast(s32[512]{0:T(512)} %param.12), dimensions={0} | broadcast | bytes 264192 | tf_op jit(solution)/shard_map/broadcast_in_dim | solution.py:373
  4.4 74.6 %shard_map.73 = f32[256,128]{1,0:T(8,128)} custom-call(bf16[4096,256]{1,0:T(8,128)(2,1)} %field.1, bf16[24576,128]{1,0:T(8,128)(2,1)} %bitcast.3, bf16[24576,128]{1,0:T(8,128)(2,1)} %bitcast.4, f32[2,128]{1,0:T(2,128)} %bitcast.5, f32[128,128]{1,0:T(8,128)} %broadcast_in_dim.4.freqs, s32[512,128]{1,0:T(8,128)} %broadcast_in_dim.5.receivers, s32[4]{0:T(128)} %floors.1), custom_call_target="tpu_custom_call" | custom-call | tf_op jit(solution)/shard_map/pallas_call | solution.py:378
  79.1 1.6 %copy.10 = f32[256,128]{1,0:T(8,128)} copy(f32[256,128]{1,0:T(8,128)} %shard_map.73) | data formatting | bytes 262144
